TPU v7x, 128 devices: a whole 4x4x4 slice. The times are simulated.
128 devices in a mesh: row: 16 (over z, y_hi, core), col: 8 (over y_lo, x).
Axes of the slice: x: 4, y: 4 (y_hi: 2, y_lo: 2; y = y_hi * 2 + y_lo), z: 4, core: 2. Of those that a mesh axis runs over, the one named last changes fastest.
Arguments:
- velocity: float32 [3, 128, 128, 128], P(None, 'row', 'col'), may hold values from -6 to 6
Outputs:
- advanced: float32 [3, 128, 128, 128], P(None, 'row', 'col')
All inputs are finite; a program needn't handle non-finite values.
Results may differ from a plain program's by a relative error of at most 0.0003.
Values sent between devices are 32-bit elements.
No kernel may reach another device: no remote copies, remote signals or barrier semaphores. Data moves between devices by JAX's collectives and lax.ppermute only.
A program may use at most 64 MiB of HBM per device.

v0:
```python
import jax
import jax.numpy as jnp
import ml_dtypes
import numpy as np
from jax import lax
from jax.experimental import pallas as pl
from jax.experimental.pallas import tpu as pltpu
from jax.sharding import PartitionSpec as P

N = 128
KX = 96
SLOTS = 32
f32, bf16 = jnp.float32, jnp.bfloat16


def owners():
    kz = np.array([1 + d // 3 for d in range(126)] + [0, 0])
    third = np.array([d % 3 for d in range(126)] + [0, 1])
    ky = np.zeros((4, SLOTS), np.int64)
    ok = np.zeros((4, SLOTS), bool)
    ky[0], ok[0] = np.arange(32), True
    ky[1], ok[1] = np.concatenate([np.arange(32, 43), np.arange(-42, -21)]), True
    ky[2, :21], ok[2, :21] = np.arange(-21, 0), True
    return kz, third, ky, ok


def split(a):
    hi = a.astype(np.float32).astype(ml_dtypes.bfloat16)
    lo = (a - hi.astype(np.float64)).astype(np.float32).astype(ml_dtypes.bfloat16)
    return hi, lo


def left(a, pad=0):
    hi, lo = split(a)
    zero = np.zeros((a.shape[0], pad), hi.dtype)
    return np.concatenate([hi, hi, lo, zero], axis=1)


def right(a):
    hi, lo = split(a)
    return np.concatenate([hi, hi, lo], axis=0)


def tables():
    kz, third, ky, ok = owners()
    cell = np.arange(N)

    def angle(a, b):
        return 2 * np.pi * (np.multiply.outer(a, b) % N) / N

    az = angle(kz, cell)
    z_fwd = left(np.concatenate([np.cos(az), -np.sin(az)], axis=0))
    z_inv = left(np.concatenate([np.cos(az.T), -np.sin(az.T)], axis=1))
    ay = angle(ky.reshape(-1), cell)
    keep = ok.reshape(-1)[:, None]
    cy, sy = np.cos(ay) * keep, np.sin(ay) * keep
    y_inv = right(np.block([[cy, sy], [-sy, cy]]))
    y_fwd = right(np.block([[cy.T, -sy.T], [sy.T, cy.T]]))
    ax = angle(np.arange(KX) - 42, cell)
    keep = (np.arange(KX) < 85)[:, None]
    cx, sx = np.cos(ax) * keep, np.sin(ax) * keep
    x_fwd = left(np.block([[cx, sx], [-sx, cx]]))
    x_inv = left(np.block([[cx.T, -sx.T], [sx.T, cx.T]]), 64)
    mask = (np.repeat(np.arange(4), SLOTS)[None, :] == third[:, None]).astype(np.float32)
    lanes = np.zeros((N, 16, N), np.float32)
    group, slot = np.repeat(np.arange(4), SLOTS), np.tile(np.arange(SLOTS), 4)
    for d in range(N):
        c = (group - third[d]) % 4
        y = ky[third[d]][slot].astype(np.float64)
        z = float(kz[d])
        good = ok[third[d]][slot] & (c < 3) & ((kz[d] > 0) | (y >= 0))
        count = np.where((kz[d] == 0) & (y == 0), 1.0, 2.0)

        def component(which):
            return (which == 0) * (c < 3), ((which == 1) * y + (which == 2) * z) * (c < 3)

        lanes[d, 0], lanes[d, 1] = component(c)
        lanes[d, 2], lanes[d, 3] = component((c + 1) % 3)
        lanes[d, 4], lanes[d, 5] = component((c + 2) % 3)
        lanes[d, 6] = y * y + z * z
        lanes[d, 7] = good * count / float(N) ** 3
        lanes[d, 8], lanes[d, 9] = c == 2, c == 0
        lanes[d, 10] = group == third[d]
    return dict(z_fwd=z_fwd, z_inv=z_inv, y_fwd=y_fwd, y_inv=y_inv, x_fwd=x_fwd, x_inv=x_inv, mask=mask, lanes=lanes)


def halves(a):
    hi = a.astype(bf16)
    return hi, (a - hi.astype(f32)).astype(bf16)


def dot(a, b):
    return jnp.dot(a, b, preferred_element_type=f32)


def apply_left(table, rows, pad=0):
    hi, lo = halves(rows)
    stack = [hi, lo, hi]
    if pad:
        stack.append(jnp.zeros((pad, rows.shape[1]), bf16))
    return dot(table, jnp.concatenate(stack, axis=0))


def apply_right(columns, table):
    hi, lo = halves(columns)
    return dot(jnp.concatenate([hi, lo, hi], axis=1), table)


def turn(a, groups):
    shift = (groups * SLOTS) % N
    return pltpu.roll(a, shift, 1) if shift else a


def swap_blocks(a):
    a = a.reshape(16, 8, N)
    row = lax.broadcasted_iota(jnp.int32, a.shape, 1)
    block = lax.broadcasted_iota(jnp.int32, a.shape, 2) // 16
    for bit in (4, 2, 1):
        same = (row & bit) == (block & bit)
        up = pltpu.roll(pltpu.roll(a, 16 * bit, 2), 8 - bit, 1)
        if bit == 4:
            a = jnp.where(same, a, up)
        else:
            down = pltpu.roll(pltpu.roll(a, N - 16 * bit, 2), bit, 1)
            a = jnp.where(same, a, jnp.where((row & bit) == 0, up, down))
    return a.reshape(N, N)


def every(ref, j, count):
    return ref[pl.ds(j, N, count), :]


def pencil_to_rows(v, z_fwd, out):
    turned = jnp.concatenate([v[c * N : (c + 1) * N, :].T for c in range(3)], axis=1)
    waves = apply_left(z_fwd[...], turned)
    for part in range(2):
        for c in range(3):
            out[pl.ds(part * 3 + c, N, 6), :] = waves[part * N : (part + 1) * N, c * N : (c + 1) * N]


def rows_to_pencil(rows, z_inv, out):
    stack = jnp.concatenate(
        [jnp.concatenate([every(rows, part * 3 + c, 6) for c in range(3)], axis=1) for part in range(2)], axis=0
    )
    cells = apply_left(z_inv[...], stack)
    for c in range(3):
        out[c * N : (c + 1) * N, :] = cells[:, c * N : (c + 1) * N].T


def y_forward(pairs, mask, table):
    spectrum = apply_right(jnp.concatenate([jnp.concatenate(p, axis=1) for p in pairs], axis=0), table)
    real, imaginary = 0.0, 0.0
    for c in range(3):
        block = spectrum[c * N : (c + 1) * N]
        real = real + turn(block[:, :N] * mask, c)
        imaginary = imaginary + turn(block[:, N:] * mask, c)
    return real, imaginary


def y_inverse(pairs, mask, table):
    stack = [
        jnp.concatenate([turn(part, -c) * mask for part in pair], axis=1) for pair in pairs for c in range(3)
    ]
    return apply_right(jnp.concatenate(stack, axis=0), table)


def slab(rows, mask, z_fwd, z_inv, y_fwd, y_inv, out):
    mask = mask[...]
    pairs = [(every(rows, 2 * j, 4), every(rows, 2 * j + 1, 4)) for j in range(2)]
    lines = y_inverse(pairs, mask, y_inv[...])
    fields = [lines[f * N : (f + 1) * N] for f in range(6)]
    stack = jnp.concatenate(
        [jnp.concatenate([a[:, part * N : (part + 1) * N] for a in fields], axis=1) for part in range(2)], axis=0
    )
    grid = apply_left(z_inv[...], stack)
    u = [grid[:, c * N : (c + 1) * N] for c in range(3)]
    w = [grid[:, (3 + c) * N : (4 + c) * N] for c in range(3)]
    product = jnp.concatenate(
        [u[1] * w[2] - u[2] * w[1], u[2] * w[0] - u[0] * w[2], u[0] * w[1] - u[1] * w[0]], axis=1
    )
    waves = apply_left(z_fwd[...], product)
    pairs = [(waves[:N, c * N : (c + 1) * N], waves[N:, c * N : (c + 1) * N]) for c in range(3)]
    real, imaginary = y_forward(pairs, mask, y_fwd[...])
    out[pl.ds(0, N, 2), :] = real
    out[pl.ds(1, N, 2), :] = imaginary


class Waves:
    def __init__(self, lanes):
        kx = (lax.broadcasted_iota(jnp.int32, (KX, N), 0) - 42).astype(f32)

        def lane(i):
            return lanes[i : i + 1, :]

        self.own = kx * lane(0) + lane(1)
        self.after = kx * lane(2) + lane(3)
        self.before = kx * lane(4) + lane(5)
        self.squared = kx * kx + lane(6)
        self.inverse = 1.0 / jnp.where(self.squared > 0, self.squared, 1.0)
        self.scale = lane(7)
        self.is_last = jnp.broadcast_to(lane(8), (KX, N)) > 0
        self.is_first = jnp.broadcast_to(lane(9), (KX, N)) > 0
        self.third = lane(10)

    def project(self, part):
        part = part * self.scale
        along = part * self.own
        along = along + turn(along, 1)
        along = along + turn(along, 2)
        return part - self.own * (along * self.inverse)

    def cross(self, part):
        two = turn(part, 2)
        after = jnp.where(self.is_last, two, turn(part, -1))
        before = jnp.where(self.is_first, two, turn(part, 1))
        return self.after * before - self.before * after


def x_forward(real, imaginary, table):
    waves = apply_left(table, jnp.concatenate([real, imaginary], axis=0))
    return waves[:KX], waves[KX:]


def send_fields(waves, state, x_inv, out):
    curl = (-waves.cross(state[1]), waves.cross(state[0]))
    stack = jnp.concatenate([jnp.concatenate([state[i], curl[i]], axis=1) for i in range(2)], axis=0)
    lines = apply_left(x_inv[...], stack, 64)
    for field in range(2):
        for part in range(2):
            out[pl.ds(2 * field + part, N, 4), :] = lines[part * N : (part + 1) * N, field * N : (field + 1) * N]


def start_modes(rows, lanes, y_fwd, x_fwd, x_inv, out, state_out):
    waves = Waves(lanes)
    planes = [swap_blocks(every(rows, j, 6)) for j in range(6)]
    real, imaginary = y_forward([(planes[c], planes[3 + c]) for c in range(3)], waves.third, y_fwd[...])
    state = [waves.project(part) for part in x_forward(real, imaginary, x_fwd[...])]
    for i in range(2):
        state_out[i * KX : (i + 1) * KX, :] = state[i]
    send_fields(waves, state, x_inv, out)


def tendency(waves, rows, x_fwd, state):
    parts = x_forward(every(rows, 0, 2), every(rows, 1, 2), x_fwd[...])
    viscous = waves.squared * (1.0 / N)
    return [waves.project(parts[i]) - viscous * state[i] for i in range(2)]


def middle_modes(rows, lanes, x_fwd, x_inv, state_in, out, middle_out, half_out):
    waves = Waves(lanes)
    state = [state_in[i * KX : (i + 1) * KX, :] for i in range(2)]
    first = tendency(waves, rows, x_fwd, state)
    step = 2.0 / N
    middle = [state[i] + step * first[i] for i in range(2)]
    for i in range(2):
        middle_out[i * KX : (i + 1) * KX, :] = middle[i]
        half_out[i * KX : (i + 1) * KX, :] = state[i] + 0.5 * step * first[i]
    send_fields(waves, middle, x_inv, out)


def final_modes(rows, lanes, x_fwd, x_inv, y_inv, middle_in, half_in, out):
    waves = Waves(lanes)
    middle = [middle_in[i * KX : (i + 1) * KX, :] for i in range(2)]
    second = tendency(waves, rows, x_fwd, middle)
    final = [half_in[i * KX : (i + 1) * KX, :] + (1.0 / N) * second[i] for i in range(2)]
    lines = apply_left(x_inv[...], jnp.concatenate(final, axis=0), 64)
    cells = y_inverse([(lines[:N], lines[N:])], waves.third, y_inv[...])
    for c in range(3):
        for part in range(2):
            plane = cells[c * N : (c + 1) * N, part * N : (part + 1) * N]
            out[pl.ds(part * 3 + c, N, 6), :] = swap_blocks(plane)


def call(kernel, outs):
    shapes = [jax.ShapeDtypeStruct(s, f32) for s in outs]
    return pl.pallas_call(kernel, out_shape=shapes if len(shapes) > 1 else shapes[0], name=kernel.__name__)


def exchange(rows):
    count = rows.shape[0] // N
    rows = rows.reshape(N, 1, count * N)
    rows = lax.all_to_all(rows, ("row", "col"), split_axis=0, concat_axis=0, tiled=True)
    return rows.reshape(N * count, N)


TABLES = tables()


def local(velocity):
    t = {name: jnp.asarray(value) for name, value in TABLES.items()}
    device = lax.axis_index("row") * lax.axis_size("col") + lax.axis_index("col")
    lanes = lax.dynamic_index_in_dim(t["lanes"], device, 0, keepdims=False)
    kept = (2 * KX, N)

    def physical(rows):
        return call(slab, [(2 * N, N)])(rows, t["mask"], t["z_fwd"], t["z_inv"], t["y_fwd"], t["y_inv"])

    shape = velocity.shape
    rows = exchange(call(pencil_to_rows, [(6 * N, N)])(velocity.reshape(3 * N, N), t["z_fwd"]))
    rows, state = call(start_modes, [(4 * N, N), kept])(rows, lanes, t["y_fwd"], t["x_fwd"], t["x_inv"])
    rows = exchange(physical(exchange(rows)))
    rows, middle, half = call(middle_modes, [(4 * N, N), kept, kept])(rows, lanes, t["x_fwd"], t["x_inv"], state)
    rows = exchange(physical(exchange(rows)))
    rows = call(final_modes, [(6 * N, N)])(rows, lanes, t["x_fwd"], t["x_inv"], t["y_inv"], middle, half)
    return call(rows_to_pencil, [(3 * N, N)])(exchange(rows), t["z_inv"]).reshape(shape)


def solution(mesh):
    placed = P(None, "row", "col", None)
    return jax.shard_map(local, mesh=mesh, in_specs=(placed,), out_specs=placed, check_vma=False)
```

profile of v0, /device:TPU:1, one launch (start us, length us, event | category | flops | bytes accessed | tf_op | source)
XLA Modules:
  0.0 127.7 jit_solution(14228996050737739842)
XLA Ops:
  0.0 2.1 %pencil_to_rows.1 = f32[768,128]{1,0:T(8,128)} custom-call(f32[384,128]{1,0:T(8,128)} %bitcast.28, bf16[256,384]{1,0:T(8,128)(2,1)} %constant.33.clone.z_fwd), custom_call_target="tpu_custom_call" | custom-call | tf_op jit(solution)/shard_map/pencil_to_rows/pallas_call | solution.py:299
  2.1 11.5 %all-to-all-start = ((f32[128,1,768]{2,1,0:T(1,128)}), f32[128,1,768]{2,1,0:T(1,128)S(1)}, u32[]{:S(2)}, u32[]{:S(2)}) async-start(f32[128,1,768]{2,1,0:T(1,128)} %bitcast.16), calls=%async_computation | async-start | bytes 786432 | tf_op jit(solution)/shard_map/all_to_all | solution.py:282
  13.6 1.3 %dynamic-slice_bitcast_fusion.lanes = f32[16,128]{1,0:T(8,128)} fusion(f32[128,16,128]{2,1,0:T(8,128)} %constant.40.clone, s32[]{:T(128)S(6)} %select_n.4), kind=kLoop, calls=%fused_computation | loop fusion | bytes 16388 | tf_op jit(solution)/shard_map/jit(dynamic_index_in_dim)/squeeze | solution.py:292
  14.9 11.3 %all-to-all-done = f32[128,1,768]{2,1,0:T(1,128)S(1)} async-done(((f32[128,1,768]{2,1,0:T(1,128)}), f32[128,1,768]{2,1,0:T(1,128)S(1)}, u32[]{:S(2)}, u32[]{:S(2)}) %all-to-all-start) | async-done | bytes 393248 | tf_op jit(solution)/shard_map/all_to_all | solution.py:282
  26.2 0.0 copy-start
  26.2 0.7 copy-done
  27.0 3.9 %start_modes.1 = (f32[512,128]{1,0:T(8,128)}, f32[192,128]{1,0:T(8,128)}) custom-call(f32[768,128]{1,0:T(8,128)} %bitcast.18, f32[16,128]{1,0:T(8,128)} %dynamic-slice_bitcast_fusion.lanes, bf16[768,256]{1,0:T(8,128)(2,1)} %constant.35.clone.y_fwd, bf16[192,768]{1,0:T(8,128)(2,1)} %constant.37.clone.x_fwd, bf16[256,640]{1,0:T(8,128)(2,1)} %constant.38.clone.x_inv), custom_call_target="tpu_custom_call" | custom-call | tf_op jit(solution)/shard_map/start_modes/pallas_call | solution.py:300
  30.8 16.3 %all_to_all.30 = f32[128,1,512]{2,1,0:T(1,128)} all-to-all(f32[128,1,512]{2,1,0:T(1,128)} %bitcast.27), channel_id=1, replica_groups=mesh['row'=16,'col'=8] {'row','col'}, dimensions={0} | all-to-all | bytes 524288 | tf_op jit(solution)/shard_map/all_to_all | solution.py:282
  47.1 3.8 %slab.2 = f32[256,128]{1,0:T(8,128)} custom-call(f32[512,128]{1,0:T(8,128)} %bitcast.21, f32[128,128]{1,0:T(8,128)} %constant.39.clone.mask, bf16[256,384]{1,0:T(8,128)(2,1)} %constant.33.clone.z_fwd, bf16[128,768]{1,0:T(8,128)(2,1)} %constant.34.clone.z_inv, bf16[768,256]{1,0:T(8,128)(2,1)} %constant.35.clone.y_fwd, bf16[768,256]{1,0:T(8,128)(2,1)} %constant.36.clone.y_inv), custom_call_target="tpu_custom_call" | custom-call | tf_op jit(solution)/shard_map/slab/pallas_call | solution.py:296
  50.9 15.4 %all_to_all.31 = f32[128,1,256]{2,1,0:T(1,128)} all-to-all(f32[128,1,256]{2,1,0:T(1,128)} %bitcast.23), channel_id=1, replica_groups=mesh['row'=16,'col'=8] {'row','col'}, dimensions={0} | all-to-all | bytes 262144 | tf_op jit(solution)/shard_map/all_to_all | solution.py:282
  66.3 2.6 %middle_modes.1 = (f32[512,128]{1,0:T(8,128)}, f32[192,128]{1,0:T(8,128)}, f32[192,128]{1,0:T(8,128)}) custom-call(f32[256,128]{1,0:T(8,128)} %bitcast.24, f32[16,128]{1,0:T(8,128)} %dynamic-slice_bitcast_fusion.lanes, bf16[192,768]{1,0:T(8,128)(2,1)} %constant.37.clone.x_fwd, bf16[256,640]{1,0:T(8,128)(2,1)} %constant.38.clone.x_inv, ...), custom_call_target="tpu_custom_call" | custom-call | tf_op jit(solution)/shard_map/middle_modes/pallas_call | solution.py:302
  69.0 16.2 %all_to_all.32 = f32[128,1,512]{2,1,0:T(1,128)} all-to-all(f32[128,1,512]{2,1,0:T(1,128)} %bitcast.26), channel_id=1, replica_groups=mesh['row'=16,'col'=8] {'row','col'}, dimensions={0} | all-to-all | bytes 524288 | tf_op jit(solution)/shard_map/all_to_all | solution.py:282
  85.2 3.8 %slab.3 = f32[256,128]{1,0:T(8,128)} custom-call(f32[512,128]{1,0:T(8,128)} %bitcast.20, f32[128,128]{1,0:T(8,128)} %constant.39.clone.mask, bf16[256,384]{1,0:T(8,128)(2,1)} %constant.33.clone.z_fwd, bf16[128,768]{1,0:T(8,128)(2,1)} %constant.34.clone.z_inv, bf16[768,256]{1,0:T(8,128)(2,1)} %constant.35.clone.y_fwd, bf16[768,256]{1,0:T(8,128)(2,1)} %constant.36.clone.y_inv), custom_call_target="tpu_custom_call" | custom-call | tf_op jit(solution)/shard_map/slab/pallas_call | solution.py:296
  89.0 15.4 %all_to_all.33 = f32[128,1,256]{2,1,0:T(1,128)} all-to-all(f32[128,1,256]{2,1,0:T(1,128)} %bitcast.22), channel_id=1, replica_groups=mesh['row'=16,'col'=8] {'row','col'}, dimensions={0} | all-to-all | bytes 262144 | tf_op jit(solution)/shard_map/all_to_all | solution.py:282
  104.4 3.6 %final_modes.1 = f32[768,128]{1,0:T(8,128)} custom-call(f32[256,128]{1,0:T(8,128)} %bitcast.25, f32[16,128]{1,0:T(8,128)} %dynamic-slice_bitcast_fusion.lanes, bf16[192,768]{1,0:T(8,128)(2,1)} %constant.37.clone.x_fwd, bf16[256,640]{1,0:T(8,128)(2,1)} %constant.38.clone.x_inv, bf16[768,256]{1,0:T(8,128)(2,1)} %constant.36.clone.y_inv, ...), custom_call_target="tpu_custom_call" | custom-call | tf_op jit(solution)/shard_map/final_modes/pallas_call | solution.py:304
  108.0 17.6 %all_to_all.34 = f32[128,1,768]{2,1,0:T(1,128)} all-to-all(f32[128,1,768]{2,1,0:T(1,128)} %bitcast.19), channel_id=1, replica_groups=mesh['row'=16,'col'=8] {'row','col'}, dimensions={0} | all-to-all | bytes 786432 | tf_op jit(solution)/shard_map/all_to_all | solution.py:282
  125.6 2.1 %rows_to_pencil.1 = f32[384,128]{1,0:T(8,128)} custom-call(f32[768,128]{1,0:T(8,128)} %bitcast.17, bf16[128,768]{1,0:T(8,128)(2,1)} %constant.34.clone.z_inv), custom_call_target="tpu_custom_call" | custom-call | tf_op jit(solution)/shard_map/rows_to_pencil/pallas_call | solution.py:305
Async XLA Ops:
  2.1 24.1 %all-to-all-start = ((f32[128,1,768]{2,1,0:T(1,128)}), f32[128,1,768]{2,1,0:T(1,128)S(1)}, u32[]{:S(2)}, u32[]{:S(2)}) async-start(f32[128,1,768]{2,1,0:T(1,128)} %bitcast.16), calls=%async_computation | async-start | bytes 786432 | tf_op jit(solution)/shard_map/all_to_all | solution.py:282
  26.2 0.7 copy-start
where the time goes:
time: 128 us
  blocking collectives  81 us (63%)
  Pallas kernels  21.9 us (17%)
  starting transfers between devices  11.5 us (9%)
  waiting for transfers between devices  11.3 us (9%)
  local copies, waits for them, and re-layouts  2.04 us (2%)
    all_to_all x5, blocking collectives, exchange(): lax.all_to_all(rows, ('row', 'col'), split_axis=0, concat_axis=0, tiled=T...  81 us
    all_to_all x1, starting transfers between devices, exchange(): lax.all_to_all(rows, ('row', 'col'), split_axis=0, concat_axis=0, tiled=T...  11.5 us
    all_to_all x1, waiting for transfers between devices, exchange(): lax.all_to_all(rows, ('row', 'col'), split_axis=0, concat_axis=0, tiled=T...  11.3 us
    pallas_call x2, Pallas kernels, physical(): call(slab, [(2 * N, N)])  7.62 us
    pallas_call x1, Pallas kernels, local(): call(start_modes, [(4 * N, N), kept])  3.85 us
    pallas_call x1, Pallas kernels, local(): call(final_modes, [(6 * N, N)])  3.58 us
    pallas_call x1, Pallas kernels, local(): call(middle_modes, [(4 * N, N), kept, kept])  2.62 us
  transfers between devices with their start and end apart: 1, of which 1 were waited for; matrix products, arithmetic and copies ran while one was open for 1% of the time, Pallas kernels for 0%

commit v1 on v0

--- a/solution.py
+++ b/solution.py
@@ -271,9 +271,10 @@
             out[pl.ds(part * 3 + c, N, 6), :] = swap_blocks(plane)
 
 
-def call(kernel, outs):
-    shapes = [jax.ShapeDtypeStruct(s, f32) for s in outs]
-    return pl.pallas_call(kernel, out_shape=shapes if len(shapes) > 1 else shapes[0], name=kernel.__name__)
+def call(kernel, outs, last=False):
+    shapes = [jax.ShapeDtypeStruct(s, f32) if last else pltpu.VMEM(s, f32) for s in outs]
+    run = pl.pallas_call(kernel, out_shape=shapes if len(shapes) > 1 else shapes[0], name=kernel.__name__)
+    return lambda *args: run(*[pltpu.with_memory_space_constraint(a, pltpu.VMEM) for a in args])
 
 
 def exchange(rows):
@@ -302,7 +303,7 @@
     rows, middle, half = call(middle_modes, [(4 * N, N), kept, kept])(rows, lanes, t["x_fwd"], t["x_inv"], state)
     rows = exchange(physical(exchange(rows)))
     rows = call(final_modes, [(6 * N, N)])(rows, lanes, t["x_fwd"], t["x_inv"], t["y_inv"], middle, half)
-    return call(rows_to_pencil, [(3 * N, N)])(exchange(rows), t["z_inv"]).reshape(shape)
+    return call(rows_to_pencil, [(3 * N, N)], last=True)(exchange(rows), t["z_inv"]).reshape(shape)
 
 
 def solution(mesh):

time: 128 us -> 112 us (0.88)
  Pallas kernels: 21.9 us -> 9.8 us
  blocking collectives: 81 us -> 75.9 us
    pallas_call x7, Pallas kernels: 21.9 us -> 9.8 us  [call(): run(*[pltpu.with_memory_space_constraint(a, pltpu.VMEM) for a in args])]
    all_to_all x5, blocking collectives: 81 us -> 75.9 us  [exchange(): lax.all_to_all(rows, ('row', 'col'), split_axis=0, concat_axis=0, tiled=T...]
where the time goes in v1:
time: 112 us
  blocking collectives  75.9 us (68%)
  waiting for transfers between devices  11.9 us (11%)
  starting transfers between devices  11.5 us (10%)
  Pallas kernels  9.8 us (9%)
  local copies, waits for them, and re-layouts  2.6 us (2%)
    all_to_all x5, blocking collectives, exchange(): lax.all_to_all(rows, ('row', 'col'), split_axis=0, concat_axis=0, tiled=T...  75.9 us
    all_to_all x1, waiting for transfers between devices, exchange(): lax.all_to_all(rows, ('row', 'col'), split_axis=0, concat_axis=0, tiled=T...  11.9 us
    all_to_all x1, starting transfers between devices, exchange(): lax.all_to_all(rows, ('row', 'col'), split_axis=0, concat_axis=0, tiled=T...  11.5 us
    pallas_call x7, Pallas kernels, call(): run(*[pltpu.with_memory_space_constraint(a, pltpu.VMEM) for a in args])  9.8 us
  transfers between devices with their start and end apart: 1, of which 1 were waited for; matrix products, arithmetic and copies ran while one was open for 1% of the time, Pallas kernels for 0%

profile of v1, /device:TPU:1, one launch (start us, length us, event | category | flops | bytes accessed | tf_op | source)
XLA Modules:
  0.0 111.7 jit_solution(486529056743522624)
XLA Ops:
  0.0 0.0 copy-start.5
  0.0 0.9 copy-done.5
  0.9 0.0 copy-start.8
  0.9 0.9 copy-done.8
  1.9 0.0 copy-start.3
  1.9 1.1 pencil_to_rows.1
  3.0 0.0 copy-start.1
  3.0 0.0 copy-start.2
  3.0 11.5 %all-to-all-start = ((f32[128,1,768]{2,1,0:T(1,128)}), f32[128,1,768]{2,1,0:T(1,128)S(1)}, u32[]{:S(2)}, u32[]{:S(2)}) async-start(f32[128,1,768]{2,1,0:T(1,128)} %bitcast.1), calls=%async_computation | async-start | bytes 786432 | tf_op jit(solution)/shard_map/all_to_all | solution.py:283
  14.5 0.7 dynamic-slice_bitcast_fusion.lanes
  15.2 11.9 %all-to-all-done = f32[128,1,768]{2,1,0:T(1,128)S(1)} async-done(((f32[128,1,768]{2,1,0:T(1,128)}), f32[128,1,768]{2,1,0:T(1,128)S(1)}, u32[]{:S(2)}, u32[]{:S(2)}) %all-to-all-start) | async-done | bytes 393248 | tf_op jit(solution)/shard_map/all_to_all | solution.py:283
  27.1 0.0 copy-done.3
  27.1 0.0 copy-done.1
  27.1 0.0 copy-done.2
  27.1 0.0 copy-start.4
  27.1 0.0 copy-start.6
  27.1 1.8 %start_modes.1 = (f32[512,128]{1,0:T(8,128)S(1)}, f32[192,128]{1,0:T(8,128)S(1)}) custom-call(f32[768,128]{1,0:T(8,128)S(1)} %bitcast.17, f32[16,128]{1,0:T(8,128)S(1)} %dynamic-slice_bitcast_fusion.lanes, bf16[768,256]{1,0:T(8,128)(2,1)S(1)} %copy-done.1, bf16[192,768]{1,0:T(8,128)(2,1)S(1)} %copy-done.3, bf16[256,640]{1,0:T(8,128)(2,1)S(1)} %copy-done.2), custom_call_target="tpu_custom_call" | custom-call | tf_op jit(solution)/shard_map/start_modes/pallas_call | solution.py:277
  28.9 0.0 copy-start
  28.9 0.0 copy-start.7
  29.0 15.2 %all_to_all.30 = f32[128,1,512]{2,1,0:T(1,128)S(1)} all-to-all(f32[128,1,512]{2,1,0:T(1,128)S(1)} %bitcast.26), channel_id=1, replica_groups=mesh['row'=16,'col'=8] {'row','col'}, dimensions={0} | all-to-all | bytes 524288 | tf_op jit(solution)/shard_map/all_to_all | solution.py:283
  44.2 0.0 copy-done.4
  44.2 0.0 copy-done.6
  44.2 0.0 copy-done
  44.2 0.0 copy-done.7
  44.2 1.8 %slab.2 = f32[256,128]{1,0:T(8,128)S(1)} custom-call(f32[512,128]{1,0:T(8,128)S(1)} %bitcast.20, f32[128,128]{1,0:T(8,128)S(1)} %copy-done.7, bf16[256,384]{1,0:T(8,128)(2,1)S(1)} %copy-done.6, bf16[128,768]{1,0:T(8,128)(2,1)S(1)} %copy-done.4, bf16[768,256]{1,0:T(8,128)(2,1)S(1)} %copy-done.1, bf16[768,256]{1,0:T(8,128)(2,1)S(1)} %copy-done), custom_call_target="tpu_custom_call" | custom-call | tf_op jit(solution)/shard_map/slab/pallas_call | solution.py:277
  46.0 14.4 %all_to_all.31 = f32[128,1,256]{2,1,0:T(1,128)S(1)} all-to-all(f32[128,1,256]{2,1,0:T(1,128)S(1)} %bitcast.22), channel_id=1, replica_groups=mesh['row'=16,'col'=8] {'row','col'}, dimensions={0} | all-to-all | bytes 262144 | tf_op jit(solution)/shard_map/all_to_all | solution.py:283
  60.3 0.8 middle_modes.1
  61.1 15.3 %all_to_all.32 = f32[128,1,512]{2,1,0:T(1,128)S(1)} all-to-all(f32[128,1,512]{2,1,0:T(1,128)S(1)} %bitcast.25), channel_id=1, replica_groups=mesh['row'=16,'col'=8] {'row','col'}, dimensions={0} | all-to-all | bytes 524288 | tf_op jit(solution)/shard_map/all_to_all | solution.py:283
  76.4 1.8 %slab.3 = f32[256,128]{1,0:T(8,128)S(1)} custom-call(f32[512,128]{1,0:T(8,128)S(1)} %bitcast.19, f32[128,128]{1,0:T(8,128)S(1)} %copy-done.7, bf16[256,384]{1,0:T(8,128)(2,1)S(1)} %copy-done.6, bf16[128,768]{1,0:T(8,128)(2,1)S(1)} %copy-done.4, bf16[768,256]{1,0:T(8,128)(2,1)S(1)} %copy-done.1, bf16[768,256]{1,0:T(8,128)(2,1)S(1)} %copy-done), custom_call_target="tpu_custom_call" | custom-call | tf_op jit(solution)/shard_map/slab/pallas_call | solution.py:277
  78.2 14.4 %all_to_all.33 = f32[128,1,256]{2,1,0:T(1,128)S(1)} all-to-all(f32[128,1,256]{2,1,0:T(1,128)S(1)} %bitcast.21), channel_id=1, replica_groups=mesh['row'=16,'col'=8] {'row','col'}, dimensions={0} | all-to-all | bytes 262144 | tf_op jit(solution)/shard_map/all_to_all | solution.py:283
  92.6 1.5 %final_modes.1 = f32[768,128]{1,0:T(8,128)S(1)} custom-call(f32[256,128]{1,0:T(8,128)S(1)} %bitcast.24, f32[16,128]{1,0:T(8,128)S(1)} %dynamic-slice_bitcast_fusion.lanes, bf16[192,768]{1,0:T(8,128)(2,1)S(1)} %copy-done.3, bf16[256,640]{1,0:T(8,128)(2,1)S(1)} %copy-done.2, bf16[768,256]{1,0:T(8,128)(2,1)S(1)} %copy-done, ...), custom_call_target="tpu_custom_call" | custom-call | tf_op jit(solution)/shard_map/final_modes/pallas_call | solution.py:277
  94.1 16.6 %all_to_all.34 = f32[128,1,768]{2,1,0:T(1,128)S(1)} all-to-all(f32[128,1,768]{2,1,0:T(1,128)S(1)} %bitcast.18), channel_id=1, replica_groups=mesh['row'=16,'col'=8] {'row','col'}, dimensions={0} | all-to-all | bytes 786432 | tf_op jit(solution)/shard_map/all_to_all | solution.py:283
  110.7 1.0 rows_to_pencil.1
Async XLA Ops:
  0.0 0.9 copy-start.5
  0.9 0.9 copy-start.8
  1.9 25.2 %copy-start.3 = (bf16[192,768]{1,0:T(8,128)(2,1)S(1)}, bf16[192,768]{1,0:T(8,128)(2,1)}, u32[]{:S(2)}) copy-start(bf16[192,768]{1,0:T(8,128)(2,1)} %constant.37.clone.x_fwd) | copy-start | bytes 884740
  3.0 24.1 %copy-start.1 = (bf16[768,256]{1,0:T(8,128)(2,1)S(1)}, bf16[768,256]{1,0:T(8,128)(2,1)}, u32[]{:S(2)}) copy-start(bf16[768,256]{1,0:T(8,128)(2,1)} %constant.35.clone.y_fwd) | copy-start | bytes 1179652
  3.0 24.1 %copy-start.2 = (bf16[256,640]{1,0:T(8,128)(2,1)S(1)}, bf16[256,640]{1,0:T(8,128)(2,1)}, u32[]{:S(2)}) copy-start(bf16[256,640]{1,0:T(8,128)(2,1)} %constant.38.clone.x_inv) | copy-start | bytes 983044
  3.0 24.1 %all-to-all-start = ((f32[128,1,768]{2,1,0:T(1,128)}), f32[128,1,768]{2,1,0:T(1,128)S(1)}, u32[]{:S(2)}, u32[]{:S(2)}) async-start(f32[128,1,768]{2,1,0:T(1,128)} %bitcast.1), calls=%async_computation | async-start | bytes 786432 | tf_op jit(solution)/shard_map/all_to_all | solution.py:283
  27.1 17.1 %copy-start.4 = (bf16[128,768]{1,0:T(8,128)(2,1)S(1)}, bf16[128,768]{1,0:T(8,128)(2,1)}, u32[]{:S(2)}) copy-start(bf16[128,768]{1,0:T(8,128)(2,1)} %constant.34.clone.z_inv) | copy-start | bytes 589828
  27.1 17.1 %copy-start.6 = (bf16[256,384]{1,0:T(8,128)(2,1)S(1)}, bf16[256,384]{1,0:T(8,128)(2,1)}, u32[]{:S(2)}) copy-start(bf16[256,384]{1,0:T(8,128)(2,1)} %constant.33.clone.z_fwd) | copy-start | bytes 589828
  28.9 15.2 %copy-start = (bf16[768,256]{1,0:T(8,128)(2,1)S(1)}, bf16[768,256]{1,0:T(8,128)(2,1)}, u32[]{:S(2)}) copy-start(bf16[768,256]{1,0:T(8,128)(2,1)} %constant.36.clone.y_inv) | copy-start | bytes 1179652
  28.9 15.2 %copy-start.7 = (f32[128,128]{1,0:T(8,128)S(1)}, f32[128,128]{1,0:T(8,128)}, u32[]{:S(2)}) copy-start(f32[128,128]{1,0:T(8,128)} %constant.39.clone.mask) | copy-start | bytes 196612

commit v2 on v1

--- a/solution.py
+++ b/solution.py
@@ -62,26 +62,7 @@
     x_fwd = left(np.block([[cx, sx], [-sx, cx]]))
     x_inv = left(np.block([[cx.T, -sx.T], [sx.T, cx.T]]), 64)
     mask = (np.repeat(np.arange(4), SLOTS)[None, :] == third[:, None]).astype(np.float32)
-    lanes = np.zeros((N, 16, N), np.float32)
-    group, slot = np.repeat(np.arange(4), SLOTS), np.tile(np.arange(SLOTS), 4)
-    for d in range(N):
-        c = (group - third[d]) % 4
-        y = ky[third[d]][slot].astype(np.float64)
-        z = float(kz[d])
-        good = ok[third[d]][slot] & (c < 3) & ((kz[d] > 0) | (y >= 0))
-        count = np.where((kz[d] == 0) & (y == 0), 1.0, 2.0)
-
-        def component(which):
-            return (which == 0) * (c < 3), ((which == 1) * y + (which == 2) * z) * (c < 3)
-
-        lanes[d, 0], lanes[d, 1] = component(c)
-        lanes[d, 2], lanes[d, 3] = component((c + 1) % 3)
-        lanes[d, 4], lanes[d, 5] = component((c + 2) % 3)
-        lanes[d, 6] = y * y + z * z
-        lanes[d, 7] = good * count / float(N) ** 3
-        lanes[d, 8], lanes[d, 9] = c == 2, c == 0
-        lanes[d, 10] = group == third[d]
-    return dict(z_fwd=z_fwd, z_inv=z_inv, y_fwd=y_fwd, y_inv=y_inv, x_fwd=x_fwd, x_inv=x_inv, mask=mask, lanes=lanes)
+    return dict(z_fwd=z_fwd, z_inv=z_inv, y_fwd=y_fwd, y_inv=y_inv, x_fwd=x_fwd, x_inv=x_inv, mask=mask)
 
 
 def halves(a):
@@ -186,21 +167,32 @@
 
 
 class Waves:
-    def __init__(self, lanes):
-        kx = (lax.broadcasted_iota(jnp.int32, (KX, N), 0) - 42).astype(f32)
-
-        def lane(i):
-            return lanes[i : i + 1, :]
-
-        self.own = kx * lane(0) + lane(1)
-        self.after = kx * lane(2) + lane(3)
-        self.before = kx * lane(4) + lane(5)
-        self.squared = kx * kx + lane(6)
+    def __init__(self):
+        device = lax.axis_index("row") * lax.axis_size("col") + lax.axis_index("col")
+        kz = jnp.where(device < 126, 1 + lax.div(device, 3), 0)
+        third = jnp.where(device < 126, lax.rem(device, 3), device - 126)
+        lane = lax.broadcasted_iota(jnp.int32, (1, N), 1)
+        group, slot = lane // SLOTS, lane % SLOTS
+        c = (group - third + 4) % 4
+        wrapped = jnp.where(slot < 11, slot + 32, slot - 53)
+        ky = jnp.where(third == 0, slot, jnp.where(third == 1, wrapped, slot - 21))
+        good = (c < 3) & ((third < 2) | (slot < 21)) & ((kz > 0) | (ky >= 0))
+        count = jnp.where((kz == 0) & (ky == 0), 1.0, 2.0)
+        kx = lax.broadcasted_iota(jnp.int32, (KX, N), 0) - 42
+
+        def component(x, y, z):
+            return jnp.where(c == x, kx, jnp.where(c == y, ky, jnp.where(c == z, kz, 0))).astype(f32)
+
+        self.own = component(0, 1, 2)
+        self.after = component(2, 0, 1)
+        self.before = component(1, 2, 0)
+        self.squared = (kx * kx + (ky * ky + kz * kz)).astype(f32)
         self.inverse = 1.0 / jnp.where(self.squared > 0, self.squared, 1.0)
-        self.scale = lane(7)
-        self.is_last = jnp.broadcast_to(lane(8), (KX, N)) > 0
-        self.is_first = jnp.broadcast_to(lane(9), (KX, N)) > 0
-        self.third = lane(10)
+        self.scale = jnp.where(good, count * (1.0 / N**3), 0.0)
+        whole = jnp.broadcast_to(c, (KX, N))
+        self.is_last = whole == 2
+        self.is_first = whole == 0
+        self.third = (group == third).astype(f32)
 
     def project(self, part):
         part = part * self.scale
@@ -230,8 +222,8 @@
             out[pl.ds(2 * field + part, N, 4), :] = lines[part * N : (part + 1) * N, field * N : (field + 1) * N]
 
 
-def start_modes(rows, lanes, y_fwd, x_fwd, x_inv, out, state_out):
-    waves = Waves(lanes)
+def start_modes(rows, y_fwd, x_fwd, x_inv, out, state_out):
+    waves = Waves()
     planes = [swap_blocks(every(rows, j, 6)) for j in range(6)]
     real, imaginary = y_forward([(planes[c], planes[3 + c]) for c in range(3)], waves.third, y_fwd[...])
     state = [waves.project(part) for part in x_forward(real, imaginary, x_fwd[...])]
@@ -246,8 +238,8 @@
     return [waves.project(parts[i]) - viscous * state[i] for i in range(2)]
 
 
-def middle_modes(rows, lanes, x_fwd, x_inv, state_in, out, middle_out, half_out):
-    waves = Waves(lanes)
+def middle_modes(rows, x_fwd, x_inv, state_in, out, middle_out, half_out):
+    waves = Waves()
     state = [state_in[i * KX : (i + 1) * KX, :] for i in range(2)]
     first = tendency(waves, rows, x_fwd, state)
     step = 2.0 / N
@@ -258,8 +250,8 @@
     send_fields(waves, middle, x_inv, out)
 
 
-def final_modes(rows, lanes, x_fwd, x_inv, y_inv, middle_in, half_in, out):
-    waves = Waves(lanes)
+def final_modes(rows, x_fwd, x_inv, y_inv, middle_in, half_in, out):
+    waves = Waves()
     middle = [middle_in[i * KX : (i + 1) * KX, :] for i in range(2)]
     second = tendency(waves, rows, x_fwd, middle)
     final = [half_in[i * KX : (i + 1) * KX, :] + (1.0 / N) * second[i] for i in range(2)]
@@ -289,8 +281,6 @@
 
 def local(velocity):
     t = {name: jnp.asarray(value) for name, value in TABLES.items()}
-    device = lax.axis_index("row") * lax.axis_size("col") + lax.axis_index("col")
-    lanes = lax.dynamic_index_in_dim(t["lanes"], device, 0, keepdims=False)
     kept = (2 * KX, N)
 
     def physical(rows):
@@ -298,11 +288,11 @@
 
     shape = velocity.shape
     rows = exchange(call(pencil_to_rows, [(6 * N, N)])(velocity.reshape(3 * N, N), t["z_fwd"]))
-    rows, state = call(start_modes, [(4 * N, N), kept])(rows, lanes, t["y_fwd"], t["x_fwd"], t["x_inv"])
+    rows, state = call(start_modes, [(4 * N, N), kept])(rows, t["y_fwd"], t["x_fwd"], t["x_inv"])
     rows = exchange(physical(exchange(rows)))
-    rows, middle, half = call(middle_modes, [(4 * N, N), kept, kept])(rows, lanes, t["x_fwd"], t["x_inv"], state)
+    rows, middle, half = call(middle_modes, [(4 * N, N), kept, kept])(rows, t["x_fwd"], t["x_inv"], state)
     rows = exchange(physical(exchange(rows)))
-    rows = call(final_modes, [(6 * N, N)])(rows, lanes, t["x_fwd"], t["x_inv"], t["y_inv"], middle, half)
+    rows = call(final_modes, [(6 * N, N)])(rows, t["x_fwd"], t["x_inv"], t["y_inv"], middle, half)
     return call(rows_to_pencil, [(3 * N, N)], last=True)(exchange(rows), t["z_inv"]).reshape(shape)
 
 

time: 112 us -> 111 us (level)
  blocking collectives: 75.9 us -> 99.8 us
  waiting for transfers between devices: 11.9 us -> 0 us
  starting transfers between devices: 11.5 us -> 0 us
    all_to_all x5 -> x6, blocking collectives: 75.9 us -> 99.8 us  [exchange(): lax.all_to_all(rows, ('row', 'col'), split_axis=0, concat_axis=0, tiled=T...]
    all_to_all x1 -> x0, waiting for transfers between devices: 11.9 us -> none  [exchange(): lax.all_to_all(rows, ('row', 'col'), split_axis=0, concat_axis=0, tiled=T...]
    all_to_all x1 -> x0, starting transfers between devices: 11.5 us -> none  [exchange(): lax.all_to_all(rows, ('row', 'col'), split_axis=0, concat_axis=0, tiled=T...]
  transfers between devices with their start and end apart: 1 -> 0, of which waited for: 1 -> 0; matrix products, arithmetic and copies ran while one was open for 1% -> 0% of each run, Pallas kernels for 0% -> 0%
where the time goes in v2:
time: 111 us
  blocking collectives  99.8 us (90%)
  Pallas kernels  9.01 us (8%)
  local copies, waits for them, and re-layouts  1.9 us (2%)
    all_to_all x6, blocking collectives, exchange(): lax.all_to_all(rows, ('row', 'col'), split_axis=0, concat_axis=0, tiled=T...  99.8 us
    pallas_call x7, Pallas kernels, call(): run(*[pltpu.with_memory_space_constraint(a, pltpu.VMEM) for a in args])  9.01 us

profile of v2, /device:TPU:1, one launch (start us, length us, event | category | flops | bytes accessed | tf_op | source)
XLA Modules:
  0.0 110.8 jit_solution(10606470004582634198)
XLA Ops:
  0.0 0.0 copy-start.5
  0.0 0.9 copy-done.5
  0.9 0.0 copy-start.8
  0.9 0.9 copy-done.8
  1.9 0.0 copy-start.3
  1.9 0.4 pencil_to_rows.1
  2.2 0.0 copy-start.1
  2.2 0.0 copy-start.2
  2.2 23.9 %all_to_all.30 = f32[128,1,768]{2,1,0:T(1,128)S(1)} all-to-all(f32[128,1,768]{2,1,0:T(1,128)S(1)} %bitcast.15), channel_id=1, replica_groups=mesh['row'=16,'col'=8] {'row','col'}, dimensions={0} | all-to-all | bytes 786432 | tf_op jit(solution)/shard_map/all_to_all | solution.py:275
  26.2 0.0 copy-done.3
  26.2 0.0 copy-done.1
  26.2 0.0 copy-done.2
  26.2 0.0 copy-start.4
  26.2 0.0 copy-start.6
  26.2 1.8 %start_modes.1 = (f32[512,128]{1,0:T(8,128)S(1)}, f32[192,128]{1,0:T(8,128)S(1)}) custom-call(f32[768,128]{1,0:T(8,128)S(1)} %bitcast.17, bf16[768,256]{1,0:T(8,128)(2,1)S(1)} %copy-done.1, bf16[192,768]{1,0:T(8,128)(2,1)S(1)} %copy-done.3, bf16[256,640]{1,0:T(8,128)(2,1)S(1)} %copy-done.2), custom_call_target="tpu_custom_call" | custom-call | tf_op jit(solution)/shard_map/start_modes/pallas_call | solution.py:269
  28.0 0.0 copy-start
  28.0 0.0 copy-start.7
  28.0 15.2 %all_to_all.31 = f32[128,1,512]{2,1,0:T(1,128)S(1)} all-to-all(f32[128,1,512]{2,1,0:T(1,128)S(1)} %bitcast.25), channel_id=1, replica_groups=mesh['row'=16,'col'=8] {'row','col'}, dimensions={0} | all-to-all | bytes 524288 | tf_op jit(solution)/shard_map/all_to_all | solution.py:275
  43.2 0.0 copy-done.4
  43.2 0.0 copy-done.6
  43.2 0.0 copy-done
  43.3 0.0 copy-done.7
  43.3 1.8 %slab.2 = f32[256,128]{1,0:T(8,128)S(1)} custom-call(f32[512,128]{1,0:T(8,128)S(1)} %bitcast.19, f32[128,128]{1,0:T(8,128)S(1)} %copy-done.7, bf16[256,384]{1,0:T(8,128)(2,1)S(1)} %copy-done.6, bf16[128,768]{1,0:T(8,128)(2,1)S(1)} %copy-done.4, bf16[768,256]{1,0:T(8,128)(2,1)S(1)} %copy-done.1, bf16[768,256]{1,0:T(8,128)(2,1)S(1)} %copy-done), custom_call_target="tpu_custom_call" | custom-call | tf_op jit(solution)/shard_map/slab/pallas_call | solution.py:269
  45.0 14.4 %all_to_all.32 = f32[128,1,256]{2,1,0:T(1,128)S(1)} all-to-all(f32[128,1,256]{2,1,0:T(1,128)S(1)} %bitcast.21), channel_id=1, replica_groups=mesh['row'=16,'col'=8] {'row','col'}, dimensions={0} | all-to-all | bytes 262144 | tf_op jit(solution)/shard_map/all_to_all | solution.py:275
  59.4 0.8 middle_modes.1
  60.2 15.3 %all_to_all.33 = f32[128,1,512]{2,1,0:T(1,128)S(1)} all-to-all(f32[128,1,512]{2,1,0:T(1,128)S(1)} %bitcast.24), channel_id=1, replica_groups=mesh['row'=16,'col'=8] {'row','col'}, dimensions={0} | all-to-all | bytes 524288 | tf_op jit(solution)/shard_map/all_to_all | solution.py:275
  75.4 1.8 %slab.3 = f32[256,128]{1,0:T(8,128)S(1)} custom-call(f32[512,128]{1,0:T(8,128)S(1)} %bitcast.18, f32[128,128]{1,0:T(8,128)S(1)} %copy-done.7, bf16[256,384]{1,0:T(8,128)(2,1)S(1)} %copy-done.6, bf16[128,768]{1,0:T(8,128)(2,1)S(1)} %copy-done.4, bf16[768,256]{1,0:T(8,128)(2,1)S(1)} %copy-done.1, bf16[768,256]{1,0:T(8,128)(2,1)S(1)} %copy-done), custom_call_target="tpu_custom_call" | custom-call | tf_op jit(solution)/shard_map/slab/pallas_call | solution.py:269
  77.2 14.4 %all_to_all.34 = f32[128,1,256]{2,1,0:T(1,128)S(1)} all-to-all(f32[128,1,256]{2,1,0:T(1,128)S(1)} %bitcast.20), channel_id=1, replica_groups=mesh['row'=16,'col'=8] {'row','col'}, dimensions={0} | all-to-all | bytes 262144 | tf_op jit(solution)/shard_map/all_to_all | solution.py:275
  91.6 1.5 %final_modes.1 = f32[768,128]{1,0:T(8,128)S(1)} custom-call(f32[256,128]{1,0:T(8,128)S(1)} %bitcast.23, bf16[192,768]{1,0:T(8,128)(2,1)S(1)} %copy-done.3, bf16[256,640]{1,0:T(8,128)(2,1)S(1)} %copy-done.2, bf16[768,256]{1,0:T(8,128)(2,1)S(1)} %copy-done, f32[192,128]{1,0:T(8,128)S(1)} %get-tuple-element.13.middle_in, f32[192,128]{1,0:T(8,128)S(1)} %get-tuple-element.14.half_in), custom_call_target="tpu_custom_call" | custom-call | tf_op jit(solution)/shard_map/final_modes/pallas_call | solution.py:269
  93.1 16.6 %all_to_all.35 = f32[128,1,768]{2,1,0:T(1,128)S(1)} all-to-all(f32[128,1,768]{2,1,0:T(1,128)S(1)} %bitcast.16), channel_id=1, replica_groups=mesh['row'=16,'col'=8] {'row','col'}, dimensions={0} | all-to-all | bytes 786432 | tf_op jit(solution)/shard_map/all_to_all | solution.py:275
  109.7 1.0 rows_to_pencil.1
Async XLA Ops:
  0.0 0.9 copy-start.5
  0.9 0.9 copy-start.8
  1.9 24.3 %copy-start.3 = (bf16[192,768]{1,0:T(8,128)(2,1)S(1)}, bf16[192,768]{1,0:T(8,128)(2,1)}, u32[]{:S(2)}) copy-start(bf16[192,768]{1,0:T(8,128)(2,1)} %constant.18.clone.x_fwd) | copy-start | bytes 884740
  2.2 23.9 %copy-start.1 = (bf16[768,256]{1,0:T(8,128)(2,1)S(1)}, bf16[768,256]{1,0:T(8,128)(2,1)}, u32[]{:S(2)}) copy-start(bf16[768,256]{1,0:T(8,128)(2,1)} %constant.16.clone.y_fwd) | copy-start | bytes 1179652
  2.2 23.9 %copy-start.2 = (bf16[256,640]{1,0:T(8,128)(2,1)S(1)}, bf16[256,640]{1,0:T(8,128)(2,1)}, u32[]{:S(2)}) copy-start(bf16[256,640]{1,0:T(8,128)(2,1)} %constant.19.clone.x_inv) | copy-start | bytes 983044
  26.2 17.1 %copy-start.4 = (bf16[128,768]{1,0:T(8,128)(2,1)S(1)}, bf16[128,768]{1,0:T(8,128)(2,1)}, u32[]{:S(2)}) copy-start(bf16[128,768]{1,0:T(8,128)(2,1)} %constant.15.clone.z_inv) | copy-start | bytes 589828
  26.2 17.1 %copy-start.6 = (bf16[256,384]{1,0:T(8,128)(2,1)S(1)}, bf16[256,384]{1,0:T(8,128)(2,1)}, u32[]{:S(2)}) copy-start(bf16[256,384]{1,0:T(8,128)(2,1)} %constant.14.clone.z_fwd) | copy-start | bytes 589828
  28.0 15.2 %copy-start = (bf16[768,256]{1,0:T(8,128)(2,1)S(1)}, bf16[768,256]{1,0:T(8,128)(2,1)}, u32[]{:S(2)}) copy-start(bf16[768,256]{1,0:T(8,128)(2,1)} %constant.17.clone.y_inv) | copy-start | bytes 1179652
  28.0 15.2 %copy-start.7 = (f32[128,128]{1,0:T(8,128)S(1)}, f32[128,128]{1,0:T(8,128)}, u32[]{:S(2)}) copy-start(f32[128,128]{1,0:T(8,128)} %constant.20.clone.mask) | copy-start | bytes 196612

commit v3 on v2

--- a/solution.py
+++ b/solution.py
@@ -111,12 +111,19 @@
     return ref[pl.ds(j, N, count), :]
 
 
-def pencil_to_rows(v, z_fwd, out):
-    turned = jnp.concatenate([v[c * N : (c + 1) * N, :].T for c in range(3)], axis=1)
-    waves = apply_left(z_fwd[...], turned)
-    for part in range(2):
-        for c in range(3):
-            out[pl.ds(part * 3 + c, N, 6), :] = waves[part * N : (part + 1) * N, c * N : (c + 1) * N]
+def pencil_to_rows(v_hbm, z_hbm, out, v, z_fwd, arrived):
+    copies = [pltpu.make_async_copy(z_hbm, z_fwd, arrived.at[3])]
+    for c in range(3):
+        part = pl.ds(c * N, N)
+        copies.append(pltpu.make_async_copy(v_hbm.at[part, :], v.at[part, :], arrived.at[c]))
+    for copy in copies:
+        copy.start()
+    copies[0].wait()
+    for c in range(3):
+        copies[1 + c].wait()
+        waves = apply_left(z_fwd[...], v[c * N : (c + 1) * N, :].T)
+        for part in range(2):
+            out[pl.ds(part * 3 + c, N, 6), :] = waves[part * N : (part + 1) * N]
 
 
 def rows_to_pencil(rows, z_inv, out):
@@ -138,17 +145,16 @@
     return real, imaginary
 
 
-def y_inverse(pairs, mask, table):
-    stack = [
-        jnp.concatenate([turn(part, -c) * mask for part in pair], axis=1) for pair in pairs for c in range(3)
-    ]
+def y_inverse(places, mask, table):
+    stack = [jnp.concatenate([turn(a, -group) * mask for a, group in pair], axis=1) for pair in places]
     return apply_right(jnp.concatenate(stack, axis=0), table)
 
 
 def slab(rows, mask, z_fwd, z_inv, y_fwd, y_inv, out):
     mask = mask[...]
-    pairs = [(every(rows, 2 * j, 4), every(rows, 2 * j + 1, 4)) for j in range(2)]
-    lines = y_inverse(pairs, mask, y_inv[...])
+    real, imaginary, rest = (every(rows, j, 3) for j in range(3))
+    places = [((real, f), (imaginary, f)) for f in range(4)] + [((rest, f), (rest, f + 2)) for f in (1, 2)]
+    lines = y_inverse(places, mask, y_inv[...])
     fields = [lines[f * N : (f + 1) * N] for f in range(6)]
     stack = jnp.concatenate(
         [jnp.concatenate([a[:, part * N : (part + 1) * N] for a in fields], axis=1) for part in range(2)], axis=0
@@ -192,6 +198,9 @@
         whole = jnp.broadcast_to(c, (KX, N))
         self.is_last = whole == 2
         self.is_first = whole == 0
+        self.is_free = whole == 3
+        lines = jnp.broadcast_to(c, (N, N))
+        self.has_rest = (lines == 1) | (lines == 2)
         self.third = (group == third).astype(f32)
 
     def project(self, part):
@@ -215,11 +224,12 @@
 
 def send_fields(waves, state, x_inv, out):
     curl = (-waves.cross(state[1]), waves.cross(state[0]))
-    stack = jnp.concatenate([jnp.concatenate([state[i], curl[i]], axis=1) for i in range(2)], axis=0)
+    both = [jnp.where(waves.is_free, turn(curl[i], 3), state[i]) for i in range(2)]
+    stack = jnp.concatenate([jnp.concatenate([both[i], curl[i]], axis=1) for i in range(2)], axis=0)
     lines = apply_left(x_inv[...], stack, 64)
-    for field in range(2):
-        for part in range(2):
-            out[pl.ds(2 * field + part, N, 4), :] = lines[part * N : (part + 1) * N, field * N : (field + 1) * N]
+    for part in range(2):
+        out[pl.ds(part, N, 3), :] = lines[part * N : (part + 1) * N, :N]
+    out[pl.ds(2, N, 3), :] = jnp.where(waves.has_rest, lines[:N, N:], turn(lines[N:, N:], 2))
 
 
 def start_modes(rows, y_fwd, x_fwd, x_inv, out, state_out):
@@ -256,7 +266,7 @@
     second = tendency(waves, rows, x_fwd, middle)
     final = [half_in[i * KX : (i + 1) * KX, :] + (1.0 / N) * second[i] for i in range(2)]
     lines = apply_left(x_inv[...], jnp.concatenate(final, axis=0), 64)
-    cells = y_inverse([(lines[:N], lines[N:])], waves.third, y_inv[...])
+    cells = y_inverse([((lines[:N], c), (lines[N:], c)) for c in range(3)], waves.third, y_inv[...])
     for c in range(3):
         for part in range(2):
             plane = cells[c * N : (c + 1) * N, part * N : (part + 1) * N]
@@ -267,6 +277,17 @@
     shapes = [jax.ShapeDtypeStruct(s, f32) if last else pltpu.VMEM(s, f32) for s in outs]
     run = pl.pallas_call(kernel, out_shape=shapes if len(shapes) > 1 else shapes[0], name=kernel.__name__)
     return lambda *args: run(*[pltpu.with_memory_space_constraint(a, pltpu.VMEM) for a in args])
+
+
+def first_call(v, z_fwd):
+    run = pl.pallas_call(
+        pencil_to_rows,
+        out_shape=pltpu.VMEM((6 * N, N), f32),
+        in_specs=[pl.BlockSpec(memory_space=pl.ANY)] * 2,
+        scratch_shapes=[pltpu.VMEM(v.shape, f32), pltpu.VMEM(z_fwd.shape, bf16), pltpu.SemaphoreType.DMA((4,))],
+        name="pencil_to_rows",
+    )
+    return run(v, z_fwd)
 
 
 def exchange(rows):
@@ -287,10 +308,10 @@
         return call(slab, [(2 * N, N)])(rows, t["mask"], t["z_fwd"], t["z_inv"], t["y_fwd"], t["y_inv"])
 
     shape = velocity.shape
-    rows = exchange(call(pencil_to_rows, [(6 * N, N)])(velocity.reshape(3 * N, N), t["z_fwd"]))
-    rows, state = call(start_modes, [(4 * N, N), kept])(rows, t["y_fwd"], t["x_fwd"], t["x_inv"])
+    rows = exchange(first_call(velocity.reshape(3 * N, N), t["z_fwd"]))
+    rows, state = call(start_modes, [(3 * N, N), kept])(rows, t["y_fwd"], t["x_fwd"], t["x_inv"])
     rows = exchange(physical(exchange(rows)))
-    rows, middle, half = call(middle_modes, [(4 * N, N), kept, kept])(rows, t["x_fwd"], t["x_inv"], state)
+    rows, middle, half = call(middle_modes, [(3 * N, N), kept, kept])(rows, t["x_fwd"], t["x_inv"], state)
     rows = exchange(physical(exchange(rows)))
     rows = call(final_modes, [(6 * N, N)])(rows, t["x_fwd"], t["x_inv"], t["y_inv"], middle, half)
     return call(rows_to_pencil, [(3 * N, N)], last=True)(exchange(rows), t["z_inv"]).reshape(shape)

time: 111 us -> 110 us (level)
  local copies, waits for them, and re-layouts: 1.9 us -> 0.04 us
  Pallas kernels: 9.01 us -> 10.8 us
  blocking collectives: 99.8 us -> 98.5 us
    pallas_call x0 -> x1, Pallas kernels: none -> 1.89 us  [first_call(): return run(v, z_fwd)]
    unnamed x18 -> x14, local copies, waits for them, and re-layouts: 1.9 us -> 0.04 us
    all_to_all x6, blocking collectives: 99.8 us -> 98.5 us  [exchange(): lax.all_to_all(rows, ('row', 'col'), split_axis=0, concat_axis=0, tiled=T...]
    pallas_call x7 -> x6, Pallas kernels: 9.01 us -> 8.92 us  [call(): run(*[pltpu.with_memory_space_constraint(a, pltpu.VMEM) for a in args])]
where the time goes in v3:
time: 110 us; the launch traced here: 109 us
  blocking collectives  98.5 us (90%)
  Pallas kernels  10.8 us (10%)
    all_to_all x6, blocking collectives, exchange(): lax.all_to_all(rows, ('row', 'col'), split_axis=0, concat_axis=0, tiled=T...  98.5 us
    pallas_call x6, Pallas kernels, call(): run(*[pltpu.with_memory_space_constraint(a, pltpu.VMEM) for a in args])  8.92 us

profile of v3, /device:TPU:1, one launch (start us, length us, event | category | flops | bytes accessed | tf_op | source)
XLA Modules:
  0.0 109.4 jit_solution(14196781234470742764)
XLA Ops:
  0.0 0.0 copy-start.3
  0.0 1.9 %pencil_to_rows.1 = f32[768,128]{1,0:T(8,128)S(1)} custom-call(f32[384,128]{1,0:T(8,128)} %bitcast.26, bf16[256,384]{1,0:T(8,128)(2,1)} %constant.14.clone.z_hbm.z_fwd), custom_call_target="tpu_custom_call" | custom-call | tf_op jit(solution)/shard_map/pencil_to_rows/pallas_call | solution.py:290
  1.9 0.0 copy-start.1
  1.9 0.0 copy-start.2
  1.9 23.9 %all_to_all.30 = f32[128,1,768]{2,1,0:T(1,128)S(1)} all-to-all(f32[128,1,768]{2,1,0:T(1,128)S(1)} %bitcast.15), channel_id=1, replica_groups=mesh['row'=16,'col'=8] {'row','col'}, dimensions={0} | all-to-all | bytes 786432 | tf_op jit(solution)/shard_map/all_to_all | solution.py:296
  25.8 0.0 copy-done.3
  25.8 0.0 copy-done.1
  25.8 0.0 copy-done.2
  25.8 0.0 copy-start.4
  25.9 0.0 copy-start.5
  25.9 0.0 copy-start.6
  25.9 1.9 %start_modes.1 = (f32[384,128]{1,0:T(8,128)S(1)}, f32[192,128]{1,0:T(8,128)S(1)}) custom-call(f32[768,128]{1,0:T(8,128)S(1)} %bitcast.17, bf16[768,256]{1,0:T(8,128)(2,1)S(1)} %copy-done.1, bf16[192,768]{1,0:T(8,128)(2,1)S(1)} %copy-done.3, bf16[256,640]{1,0:T(8,128)(2,1)S(1)} %copy-done.2), custom_call_target="tpu_custom_call" | custom-call | tf_op jit(solution)/shard_map/start_modes/pallas_call | solution.py:279
  27.8 0.0 copy-start
  27.9 14.5 %all_to_all.31 = f32[128,1,384]{2,1,0:T(1,128)S(1)} all-to-all(f32[128,1,384]{2,1,0:T(1,128)S(1)} %bitcast.25), channel_id=1, replica_groups=mesh['row'=16,'col'=8] {'row','col'}, dimensions={0} | all-to-all | bytes 393216 | tf_op jit(solution)/shard_map/all_to_all | solution.py:296
  42.4 0.0 copy-done.4
  42.4 0.0 copy-done.5
  42.4 0.0 copy-done.6
  42.4 0.0 copy-done
  42.4 1.8 %slab.2 = f32[256,128]{1,0:T(8,128)S(1)} custom-call(f32[384,128]{1,0:T(8,128)S(1)} %bitcast.19, f32[128,128]{1,0:T(8,128)S(1)} %copy-done.6, bf16[256,384]{1,0:T(8,128)(2,1)S(1)} %copy-done.5, bf16[128,768]{1,0:T(8,128)(2,1)S(1)} %copy-done.4, bf16[768,256]{1,0:T(8,128)(2,1)S(1)} %copy-done.1, bf16[768,256]{1,0:T(8,128)(2,1)S(1)} %copy-done), custom_call_target="tpu_custom_call" | custom-call | tf_op jit(solution)/shard_map/slab/pallas_call | solution.py:279
  44.2 14.4 %all_to_all.32 = f32[128,1,256]{2,1,0:T(1,128)S(1)} all-to-all(f32[128,1,256]{2,1,0:T(1,128)S(1)} %bitcast.21), channel_id=1, replica_groups=mesh['row'=16,'col'=8] {'row','col'}, dimensions={0} | all-to-all | bytes 262144 | tf_op jit(solution)/shard_map/all_to_all | solution.py:296
  58.6 0.9 middle_modes.1
  59.5 14.6 %all_to_all.33 = f32[128,1,384]{2,1,0:T(1,128)S(1)} all-to-all(f32[128,1,384]{2,1,0:T(1,128)S(1)} %bitcast.24), channel_id=1, replica_groups=mesh['row'=16,'col'=8] {'row','col'}, dimensions={0} | all-to-all | bytes 393216 | tf_op jit(solution)/shard_map/all_to_all | solution.py:296
  74.1 1.8 %slab.3 = f32[256,128]{1,0:T(8,128)S(1)} custom-call(f32[384,128]{1,0:T(8,128)S(1)} %bitcast.18, f32[128,128]{1,0:T(8,128)S(1)} %copy-done.6, bf16[256,384]{1,0:T(8,128)(2,1)S(1)} %copy-done.5, bf16[128,768]{1,0:T(8,128)(2,1)S(1)} %copy-done.4, bf16[768,256]{1,0:T(8,128)(2,1)S(1)} %copy-done.1, bf16[768,256]{1,0:T(8,128)(2,1)S(1)} %copy-done), custom_call_target="tpu_custom_call" | custom-call | tf_op jit(solution)/shard_map/slab/pallas_call | solution.py:279
  75.9 14.4 %all_to_all.34 = f32[128,1,256]{2,1,0:T(1,128)S(1)} all-to-all(f32[128,1,256]{2,1,0:T(1,128)S(1)} %bitcast.20), channel_id=1, replica_groups=mesh['row'=16,'col'=8] {'row','col'}, dimensions={0} | all-to-all | bytes 262144 | tf_op jit(solution)/shard_map/all_to_all | solution.py:296
  90.3 1.5 %final_modes.1 = f32[768,128]{1,0:T(8,128)S(1)} custom-call(f32[256,128]{1,0:T(8,128)S(1)} %bitcast.23, bf16[192,768]{1,0:T(8,128)(2,1)S(1)} %copy-done.3, bf16[256,640]{1,0:T(8,128)(2,1)S(1)} %copy-done.2, bf16[768,256]{1,0:T(8,128)(2,1)S(1)} %copy-done, f32[192,128]{1,0:T(8,128)S(1)} %get-tuple-element.13.middle_in, f32[192,128]{1,0:T(8,128)S(1)} %get-tuple-element.14.half_in), custom_call_target="tpu_custom_call" | custom-call | tf_op jit(solution)/shard_map/final_modes/pallas_call | solution.py:279
  91.8 16.6 %all_to_all.35 = f32[128,1,768]{2,1,0:T(1,128)S(1)} all-to-all(f32[128,1,768]{2,1,0:T(1,128)S(1)} %bitcast.16), channel_id=1, replica_groups=mesh['row'=16,'col'=8] {'row','col'}, dimensions={0} | all-to-all | bytes 786432 | tf_op jit(solution)/shard_map/all_to_all | solution.py:296
  108.4 1.0 rows_to_pencil.1
Async XLA Ops:
  0.0 25.8 %copy-start.3 = (bf16[192,768]{1,0:T(8,128)(2,1)S(1)}, bf16[192,768]{1,0:T(8,128)(2,1)}, u32[]{:S(2)}) copy-start(bf16[192,768]{1,0:T(8,128)(2,1)} %constant.18.clone.x_fwd) | copy-start | bytes 884740
  1.9 23.9 %copy-start.1 = (bf16[768,256]{1,0:T(8,128)(2,1)S(1)}, bf16[768,256]{1,0:T(8,128)(2,1)}, u32[]{:S(2)}) copy-start(bf16[768,256]{1,0:T(8,128)(2,1)} %constant.16.clone.y_fwd) | copy-start | bytes 1179652
  1.9 23.9 %copy-start.2 = (bf16[256,640]{1,0:T(8,128)(2,1)S(1)}, bf16[256,640]{1,0:T(8,128)(2,1)}, u32[]{:S(2)}) copy-start(bf16[256,640]{1,0:T(8,128)(2,1)} %constant.19.clone.x_inv) | copy-start | bytes 983044
  25.8 16.6 %copy-start.4 = (bf16[128,768]{1,0:T(8,128)(2,1)S(1)}, bf16[128,768]{1,0:T(8,128)(2,1)}, u32[]{:S(2)}) copy-start(bf16[128,768]{1,0:T(8,128)(2,1)} %constant.15.clone.z_inv) | copy-start | bytes 589828
  25.9 16.5 %copy-start.5 = (bf16[256,384]{1,0:T(8,128)(2,1)S(1)}, bf16[256,384]{1,0:T(8,128)(2,1)}, u32[]{:S(2)}) copy-start(bf16[256,384]{1,0:T(8,128)(2,1)} %constant.14.clone.z_hbm.z_fwd) | copy-start | bytes 589828
  25.9 16.5 %copy-start.6 = (f32[128,128]{1,0:T(8,128)S(1)}, f32[128,128]{1,0:T(8,128)}, u32[]{:S(2)}) copy-start(f32[128,128]{1,0:T(8,128)} %constant.20.clone.mask) | copy-start | bytes 196612
  27.8 14.6 %copy-start = (bf16[768,256]{1,0:T(8,128)(2,1)S(1)}, bf16[768,256]{1,0:T(8,128)(2,1)}, u32[]{:S(2)}) copy-start(bf16[768,256]{1,0:T(8,128)(2,1)} %constant.17.clone.y_inv) | copy-start | bytes 1179652
